TPU v7x, 512 devices: a whole 4x8x8 slice. The times are simulated.
512 devices in a mesh: row: 16 (over x, y_hi, core), col: 32 (over y_lo, z).
Axes of the slice: x: 4, y: 8 (y_hi: 2, y_lo: 4; y = y_hi * 4 + y_lo), z: 8, core: 2. Of those that a mesh axis runs over, the one named last changes fastest.
Arguments:
- resident: float32 [12288, 12288], P('row', 'col')
- factor: float32 [1, 12288, 512], P(None, 'col', 'row'), may hold values from -0.078125 to 0.078125
- dinv: float32 [1, 512, 512], P(None, 'col')
- panel_cols: int32 [1, 512], replicated, may hold values from 0 to 12287, as said below
- row_lists: int32 [1, 6144], replicated, may hold values from 0 to 12287, as said below
Outputs:
- inverse_out: float32 [12288, 12288], P('row', 'col')
Inputs may be any that keep to these rules, and one draw needn't show every extreme that they name: The entries of panel_cols are distinct positions. The resident array and every dinv[k] are symmetric. Each row_lists[k] holds distinct positions, none of them in panel_cols[j] for any j <= k.
All inputs are finite; a program needn't handle non-finite values.
Results may differ from a plain program's by a relative error of at most 0.0001.
Values sent between devices are 32-bit elements; how exact they have to be, the bound alone decides.
No kernel may reach another device: no remote copies, remote signals or barrier semaphores. Data moves between devices by JAX's collectives and lax.ppermute only.
A program may use at most 64 MiB of HBM per device.

v0:
```python
import jax
import jax.numpy as jnp
from jax import lax
from jax.sharding import Mesh
from jax.sharding import PartitionSpec as P

ROW = ("row_0", "row_1", "row_2")


def split_up(shard, dim, count):
    shape = shard.shape
    blocks = shard.reshape(*shape[:dim], count, shape[dim] // count, *shape[dim + 1 :])
    return jnp.moveaxis(blocks, dim, 0)


def sum_at_owner(shard, axis, dim):
    count = lax.axis_size(axis)
    blocks = lax.all_to_all(split_up(shard, dim, count), axis, 0, 0, tiled=True)
    return jnp.sum(blocks, axis=0)


def in_order(blocks, dim):
    shape = list(blocks.shape[1:])
    shape[dim] *= blocks.shape[0]
    return jnp.moveaxis(blocks, 0, dim).reshape(shape)


def sent_to_all(shard, axis):
    copies = jnp.broadcast_to(shard, (lax.axis_size(axis), *shard.shape))
    return lax.all_to_all(copies, axis, split_axis=0, concat_axis=0, tiled=True)


def gathered_copies(shard, axis, dim):
    return in_order(sent_to_all(shard, axis), dim)


def padded_to(lines, count):
    spare = -len(lines) % count
    return jnp.pad(lines, [(0, spare)] + [(0, 0)] * (lines.ndim - 1))


def gather_axes(shard, axes, dim):
    far, near = axes
    initial = sent_to_all(shard, far)
    blocks = jnp.swapaxes(sent_to_all(initial, near), 0, 1)
    return in_order(blocks.reshape(-1, *shard.shape), dim)


def summed_rows(shard, axes, dim):
    far, near = axes
    blocks = split_up(shard, dim, lax.axis_size(far))
    nearer = sum_at_owner(blocks, near, dim + 1)
    arrived = lax.all_to_all(nearer, far, split_axis=0, concat_axis=0, tiled=True)
    return arrived.sum(axis=0)


def sum_by_parts(shard, axes):
    lines = shard.reshape(-1, shard.shape[-1])
    padded = padded_to(lines, lax.axis_size(axes[0]) * lax.axis_size(axes[1]))
    whole = gather_axes(summed_rows(padded, axes, 0), axes, 0)
    return lax.slice_in_dim(whole, 0, len(lines)).reshape(shard.shape)


def sum_by_parts_2(shard, axes):
    lines = shard.reshape(-1, shard.shape[-1])
    own = sum_at_owner(padded_to(lines, lax.axis_size(axes)), axes, 0)
    whole = gathered_copies(own, axes, 0)
    return whole[: len(lines)].reshape(shard.shape)


def on_device(resident, factor, dinv, panel_cols, row_lists):
    highest = lax.Precision.HIGHEST
    row_count = lax.axis_size(ROW)
    col_count = lax.axis_size("col")
    ratio = col_count // row_count
    row_block, col_block = resident.shape
    total = row_block * row_count
    width = panel_cols.shape[1]
    dinv_rows = dinv.shape[1]
    row_pos = lax.axis_index(ROW)
    col_pos = lax.axis_index("col")
    row_ids = row_pos * row_block + jnp.arange(row_block, dtype=jnp.int32)
    col_ids = col_pos * col_block + jnp.arange(col_block, dtype=jnp.int32)
    matrix = resident
    for panel in reversed(range(factor.shape[0])):
        in_rows = jnp.zeros((total,), jnp.float32).at[row_lists[panel]].set(1.0)
        panel_map = (
            jnp.full((total,), -1, jnp.int32)
            .at[panel_cols[panel]]
            .set(jnp.arange(width, dtype=jnp.int32))
        )
        col_mask = in_rows[col_ids]
        gathered = lax.all_gather(factor[panel], ROW, axis=1, tiled=True)
        lower_cols = gathered * col_mask[:, None]
        partial_value = jnp.dot(matrix, lower_cols, precision=highest)
        shares = sum_at_owner(-partial_value, "col", 0)
        product_rows = gathered_copies(shares, "col", 0)
        owner = col_pos // ratio
        offset = col_pos % ratio * col_block
        mine = lax.dynamic_slice_in_dim(product_rows, offset, col_block, 0)
        masked = jnp.where(row_pos == owner, mine, jnp.zeros_like(mine))
        product_cols = sum_by_parts(masked, (("row_0", "row_1"), "row_2"))
        placed = lax.dynamic_update_slice(
            jnp.zeros((width, width), jnp.float32), dinv[panel], (col_pos * dinv_rows, 0)
        )
        gram_term = jnp.dot(lower_cols.T, product_cols, precision=highest)
        diagonal = sum_by_parts_2(placed - gram_term, "col")
        row_slot = panel_map[row_ids]
        col_slot = panel_map[col_ids]
        row_safe = jnp.maximum(row_slot, 0)
        col_safe = jnp.maximum(col_slot, 0)
        row_in = in_rows[row_ids] > 0.5
        col_in = col_mask > 0.5
        row_panel = row_slot >= 0
        col_panel = col_slot >= 0
        below = jnp.take(product_rows, col_safe, axis=1)
        beside = jnp.take(product_cols, row_safe, axis=1).T
        corner = jnp.take(jnp.take(diagonal, row_safe, axis=0), col_safe, axis=1)
        matrix = jnp.where(
            row_panel[:, None] & col_panel[None, :],
            corner,
            jnp.where(
                row_panel[:, None] & col_in[None, :],
                beside,
                jnp.where(row_in[:, None] & col_panel[None, :], below, matrix),
            ),
        )
    return matrix


def solution(mesh):
    finer = Mesh(
        mesh.devices.reshape(4, 2, 2, mesh.shape["col"]), ("row_0", "row_1", "row_2", "col")
    )
    return jax.shard_map(
        on_device,
        mesh=finer,
        in_specs=(P(ROW, "col"), P(None, "col", ROW), P(None, "col", None), P(), P()),
        out_specs=P(ROW, "col"),
        check_vma=False,
    )
```

profile of v0, /device:TPU:16, one launch (start us, length us, event | category | flops | bytes accessed | tf_op | source)
XLA Modules:
  0.0 302.5 jit_solution(6073321219527905925)
XLA Ops:
  0.0 0.8 compare_select_fusion
  0.8 33.7 %all-gather = f32[1,384,512]{1,2,0:T(8,128)S(1)} all-gather(f32[1,384,32]{1,2,0:T(8,128)} %param.8), channel_id=2, replica_groups=mesh['row_0'=4,'row_1'=2,'row_2'=2,'col'=32] {'row_0','row_1','row_2'}, dimensions={2}, use_global_device_ids=true | all-gather | bytes 835584 | tf_op jit(solution)/shard_map/all_gather | solution.py:93
  34.5 0.0 copy-start.1
  34.5 23.0 %scatter_custom_fusion.1 = f32[12288]{0:T(1024)S(1)} fusion(s32[6144]{0:T(1024)S(1)} %bitcast.42, f32[6144]{0:T(1024)S(1)} %broadcast.138, f32[]{:T(128)} %constant.105.clone.1), kind=kCustom, calls=%fused_computation.22 | custom fusion | bytes 49156 | tf_op jit(solution)/shard_map/scatter | solution.py:86
  57.5 2.5 gather_fusion.2
  60.1 0.0 copy-done.1
  60.1 3.9 %negate_bitcast_fusion = f32[768,512]{0,1:T(8,128)} fusion(f32[768,384]{1,0:T(8,128)S(1)} %copy-done.1, f32[1,384,512]{1,2,0:T(8,128)S(1)} %all-gather, f32[384]{0:T(512)S(1)} %gather_fusion.2), kind=kOutput, calls=%fused_computation.10 | convolution fusion | flops 1812529152 | bytes 3540480 | tf_op jit(solution)/shard_map/dot_general | solution.py:95
  63.9 1.9 copy.26
  65.8 58.1 %all_to_all.40 = f32[32,24,512]{2,1,0:T(8,128)} all-to-all(f32[32,24,512]{2,1,0:T(8,128)S(1)} %bitcast.39), channel_id=1, replica_groups=mesh['row_0'=4,'row_1'=2,'row_2'=2,'col'=32] {'col'}, dimensions={0} | all-to-all | bytes 3145728 | tf_op jit(solution)/shard_map/all_to_all | solution.py:18
  123.9 1.5 reduce_sum.36
  125.4 1.3 broadcast_in_dim.74
  126.8 6.6 %all-to-all-start.1 = ((f32[32,24,512]{2,1,0:T(8,128)}), f32[32,24,512]{2,1,0:T(8,128)S(1)}, u32[]{:S(2)}, u32[]{:S(2)}) async-start(f32[32,24,512]{2,1,0:T(8,128)} %broadcast_in_dim.74), calls=%async_computation.1 | async-start | bytes 3145728 | tf_op jit(solution)/shard_map/all_to_all | solution.py:30
  133.4 39.3 %all-to-all-done.1 = f32[32,24,512]{2,1,0:T(8,128)S(1)} async-done(((f32[32,24,512]{2,1,0:T(8,128)}), f32[32,24,512]{2,1,0:T(8,128)S(1)}, u32[]{:S(2)}, u32[]{:S(2)}) %all-to-all-start.1) | async-done | bytes 1572896 | tf_op jit(solution)/shard_map/all_to_all | solution.py:30
  172.7 0.0 copy-start
  172.7 0.1 dynamic-slice_select_fusion
  172.8 0.1 copy.27
  172.9 1.0 copy-done
  173.9 4.4 %all_to_all.41 = f32[2,8,24,512]{3,2,1,0:T(8,128)S(1)} all-to-all(f32[2,8,24,512]{3,2,1,0:T(8,128)S(1)} %copy.27), channel_id=1, replica_groups=mesh['row_0'=4,'row_1'=2,'row_2'=2,'col'=32] {'row_2'}, dimensions={0} | all-to-all | bytes 1572864 | tf_op jit(solution)/shard_map/all_to_all | solution.py:18
  178.2 0.1 reduce_sum.37
  178.3 20.3 %all_to_all.42 = f32[8,24,512]{2,1,0:T(8,128)S(1)} all-to-all(f32[8,24,512]{2,1,0:T(8,128)S(1)} %reduce_sum.37), channel_id=1, replica_groups=mesh['row_0'=4,'row_1'=2,'row_2'=2,'col'=32] {'row_0','row_1'}, dimensions={0} | all-to-all | bytes 786432 | tf_op jit(solution)/shard_map/all_to_all | solution.py:53
  198.6 0.0 copy-start.4
  198.6 0.8 broadcast_in_dim.76
  199.4 3.5 %all-to-all-start.4 = ((f32[8,24,512]{2,1,0:T(8,128)}), f32[8,24,512]{2,1,0:T(8,128)S(1)}, u32[]{:S(2)}, u32[]{:S(2)}) async-start(f32[8,24,512]{2,1,0:T(8,128)} %broadcast_in_dim.76), calls=%async_computation.4 | async-start | bytes 786432 | tf_op jit(solution)/shard_map/all_to_all | solution.py:30
  202.9 0.1 broadcast_in_dim.71
  203.0 0.0 copy-done.4
  203.0 14.7 %all-to-all-done.4 = f32[8,24,512]{2,1,0:T(8,128)S(1)} async-done(((f32[8,24,512]{2,1,0:T(8,128)}), f32[8,24,512]{2,1,0:T(8,128)S(1)}, u32[]{:S(2)}, u32[]{:S(2)}) %all-to-all-start.4) | async-done | bytes 393248 | tf_op jit(solution)/shard_map/all_to_all | solution.py:30
  217.7 0.1 broadcast_in_dim.77
  217.8 4.4 %all_to_all.43 = f32[2,8,24,512]{3,2,1,0:T(8,128)S(1)} all-to-all(f32[2,8,24,512]{3,2,1,0:T(8,128)S(1)} %broadcast_in_dim.77), channel_id=1, replica_groups=mesh['row_0'=4,'row_1'=2,'row_2'=2,'col'=32] {'row_2'}, dimensions={0} | all-to-all | bytes 1572864 | tf_op jit(solution)/shard_map/all_to_all | solution.py:30
  222.2 0.1 copy.28
  222.2 1.8 convolution_subtract_fusion
  224.1 31.9 %all_to_all.44 = f32[32,16,512]{2,1,0:T(8,128)S(1)} all-to-all(f32[32,16,512]{2,1,0:T(8,128)S(1)} %bitcast.40), channel_id=1, replica_groups=mesh['row_0'=4,'row_1'=2,'row_2'=2,'col'=32] {'col'}, dimensions={0} | all-to-all | bytes 2097152 | tf_op jit(solution)/shard_map/all_to_all | solution.py:18
  256.0 0.1 reduce_sum.39
  256.1 1.1 broadcast_in_dim.78
  257.2 0.0 copy-start.5
  257.2 6.0 %all-to-all-start.7 = ((f32[32,16,512]{2,1,0:T(8,128)}), f32[32,16,512]{2,1,0:T(8,128)S(1)}, u32[]{:S(2)}, u32[]{:S(2)}) async-start(f32[32,16,512]{2,1,0:T(8,128)} %broadcast_in_dim.78), calls=%async_computation.7 | async-start | bytes 2097152 | tf_op jit(solution)/shard_map/all_to_all | solution.py:30
  263.2 0.0 copy-done.5
  263.3 2.6 scatter_custom_fusion
  265.9 2.5 gather_fusion.1
  268.5 4.5 %gather_fusion = s32[768]{0:T(1024)S(1)} fusion(s32[12288]{0:T(1024)S(1)} %scatter_custom_fusion, s32[1024]{0:T(1024)S(1)} %pad_clamp_fusion.3), kind=kCustom, calls=%fused_computation.2 | custom fusion | bytes 9216 | tf_op jit(solution)/shard_map/gather | solution.py:108
  273.0 0.0 copy-start.2
  273.0 4.5 %gather_fusion.5 = f32[768]{0:T(1024)S(1)} fusion(f32[12288]{0:T(1024)S(1)} %scatter_custom_fusion.1, s32[1024]{0:T(1024)S(1)} %pad_clamp_fusion.3), kind=kCustom, calls=%fused_computation.7 | custom fusion | bytes 9216 | tf_op jit(solution)/shard_map/gather | solution.py:112
  277.5 0.0 copy-done.2
  277.5 1.4 copy.33
  278.9 1.9 copy.32
  280.8 2.5 gather_fusion.7
  283.3 0.3 copy.30
  283.6 2.1 gather_fusion.4
  285.7 1.4 copy.31
  287.1 3.7 %all-to-all-done.7 = f32[32,16,512]{2,1,0:T(8,128)S(1)} async-done(((f32[32,16,512]{2,1,0:T(8,128)}), f32[32,16,512]{2,1,0:T(8,128)S(1)}, u32[]{:S(2)}, u32[]{:S(2)}) %all-to-all-start.7) | async-done | bytes 1048608 | tf_op jit(solution)/shard_map/all_to_all | solution.py:30
  290.8 3.1 %gather_fusion.3 = f32[768,512]{1,0:T(8,128)} fusion(f32[512,512]{1,0:T(8,128)S(1)} %bitcast.34, s32[1024]{0:T(1024)S(1)} %pad_clamp_fusion.1), kind=kCustom, calls=%fused_computation.5 | custom fusion | bytes 3148800 | tf_op jit(solution)/shard_map/jit(_take)/gather | solution.py:118
  294.0 1.6 broadcast_select_fusion
  295.6 0.5 copy.29
  296.0 0.0 copy-start.3
  296.0 2.5 gather_fusion.6
  298.5 0.0 copy-done.3
  298.5 2.6 fusion.1
  301.1 1.4 copy.34
  (17 shorter events, 0.2 us)
Async XLA Ops:
  34.5 25.6 %copy-start.1 = (f32[768,384]{1,0:T(8,128)S(1)}, f32[768,384]{1,0:T(8,128)}, u32[]{:S(2)}) copy-start(f32[768,384]{1,0:T(8,128)} %param.7) | copy-start | bytes 3538948
  126.8 46.0 %all-to-all-start.1 = ((f32[32,24,512]{2,1,0:T(8,128)}), f32[32,24,512]{2,1,0:T(8,128)S(1)}, u32[]{:S(2)}, u32[]{:S(2)}) async-start(f32[32,24,512]{2,1,0:T(8,128)} %broadcast_in_dim.74), calls=%async_computation.1 | async-start | bytes 3145728 | tf_op jit(solution)/shard_map/all_to_all | solution.py:30
  172.7 1.2 copy-start
  198.6 4.4 %copy-start.4 = (f32[1,16,512]{2,1,0:T(8,128)S(1)}, f32[1,16,512]{2,1,0:T(8,128)}, u32[]{:S(2)}) copy-start(f32[1,16,512]{2,1,0:T(8,128)} %param.9) | copy-start | bytes 98308
  199.4 18.3 %all-to-all-start.4 = ((f32[8,24,512]{2,1,0:T(8,128)}), f32[8,24,512]{2,1,0:T(8,128)S(1)}, u32[]{:S(2)}, u32[]{:S(2)}) async-start(f32[8,24,512]{2,1,0:T(8,128)} %broadcast_in_dim.76), calls=%async_computation.4 | async-start | bytes 786432 | tf_op jit(solution)/shard_map/all_to_all | solution.py:30
  257.2 6.1 %copy-start.5 = (s32[1,512]{1,0:T(1,128)S(1)}, s32[1,512]{1,0:T(1,128)}, u32[]{:S(2)}) copy-start(s32[1,512]{1,0:T(1,128)} %param.10) | copy-start | bytes 6148
  257.2 33.7 %all-to-all-start.7 = ((f32[32,16,512]{2,1,0:T(8,128)}), f32[32,16,512]{2,1,0:T(8,128)S(1)}, u32[]{:S(2)}, u32[]{:S(2)}) async-start(f32[32,16,512]{2,1,0:T(8,128)} %broadcast_in_dim.78), calls=%async_computation.7 | async-start | bytes 2097152 | tf_op jit(solution)/shard_map/all_to_all | solution.py:30
  273.0 4.5 %copy-start.2 = (f32[768,384]{1,0:T(8,128)S(1)}, f32[768,384]{1,0:T(8,128)}, u32[]{:S(2)}) copy-start(f32[768,384]{1,0:T(8,128)} %param.7) | copy-start | bytes 3538948
  296.0 2.5 copy-start.3
where the time goes:
time: 303 us
  blocking collectives  153 us (50%)
  local copies, waits for them, and re-layouts  63.1 us (21%)
  waiting for transfers between devices  57.8 us (19%)
  starting transfers between devices  16.1 us (5%)
  other arithmetic  6.79 us (2%)
  matrix products  5.68 us (2%)
    all_to_all x3, blocking collectives, sum_at_owner(): blocks = lax.all_to_all(split_up(shard, dim, count), axis, 0, 0, tiled=True)  94.4 us
    all_to_all x3, waiting for transfers between devices, sent_to_all(): return lax.all_to_all(copies, axis, split_axis=0, concat_axis=0, tiled=True)  57.8 us
    all_gather x1, blocking collectives, on_device(): gathered = lax.all_gather(factor[panel], ROW, axis=1, tiled=True)  33.7 us
    scatter x1, local copies, waits for them, and re-layouts, on_device(): in_rows = jnp.zeros((total,), jnp.float32).at[row_lists[panel]].set(1.0)  23 us
    all_to_all x1, blocking collectives, summed_rows(): lax.all_to_all(nearer, far, split_axis=0, concat_axis=0, tiled=True)  20.3 us
    all_to_all x3, starting transfers between devices, sent_to_all(): return lax.all_to_all(copies, axis, split_axis=0, concat_axis=0, tiled=True)  16.1 us
  transfers between devices with their start and end apart: 3, of which 3 were waited for; matrix products, arithmetic and copies ran while one was open for 8% of the time, Pallas kernels for 0%

commit v1 on v0

--- a/solution.py
+++ b/solution.py
@@ -90,7 +90,11 @@
             .set(jnp.arange(width, dtype=jnp.int32))
         )
         col_mask = in_rows[col_ids]
-        gathered = lax.all_gather(factor[panel], ROW, axis=1, tiled=True)
+        block = factor[panel]
+        size = lax.axis_size(ROW)
+        parts = jnp.stack([block for _ in range(size)])
+        parts = lax.all_to_all(parts, ROW, split_axis=0, concat_axis=0)
+        gathered = jnp.concatenate(parts, axis=1)
         lower_cols = gathered * col_mask[:, None]
         partial_value = jnp.dot(matrix, lower_cols, precision=highest)
         shares = sum_at_owner(-partial_value, "col", 0)

time: 303 us -> 278 us (0.917)
  blocking collectives: 153 us -> 121 us
  starting transfers between devices: 16.1 us -> 23.8 us
  local copies, waits for them, and re-layouts: 63.1 us -> 68.4 us
    all_gather x1 -> x0, blocking collectives: 33.7 us -> none  [on_device(): gathered = lax.all_gather(factor[panel], ROW, axis=1, tiled=True)]
    all_to_all x0 -> x1, starting transfers between devices: none -> 7.87 us  [on_device(): parts = lax.all_to_all(parts, ROW, split_axis=0, concat_axis=0)]
    all_to_all x1, blocking collectives: 20.3 us -> 24.4 us  [summed_rows(): lax.all_to_all(nearer, far, split_axis=0, concat_axis=0, tiled=True)]
    all_to_all x3, waiting for transfers between devices: 57.8 us -> 54.5 us  [sent_to_all(): return lax.all_to_all(copies, axis, split_axis=0, concat_axis=0, tiled=True)]
  transfers between devices with their start and end apart: 3 -> 4, of which waited for: 3 -> 4; matrix products, arithmetic and copies ran while one was open for 8% -> 19% of each run, Pallas kernels for 0% -> 0%
where the time goes in v1:
time: 278 us
  blocking collectives  121 us (44%)
  local copies, waits for them, and re-layouts  68.4 us (25%)
  waiting for transfers between devices  54.8 us (20%)
  starting transfers between devices  23.8 us (9%)
  other arithmetic  4.88 us (2%)
  matrix products  4.51 us (2%)
    all_to_all x3, blocking collectives, sum_at_owner(): blocks = lax.all_to_all(split_up(shard, dim, count), axis, 0, 0, tiled=True)  91.9 us
    all_to_all x3, waiting for transfers between devices, sent_to_all(): return lax.all_to_all(copies, axis, split_axis=0, concat_axis=0, tiled=True)  54.5 us
    all_to_all x1, blocking collectives, summed_rows(): lax.all_to_all(nearer, far, split_axis=0, concat_axis=0, tiled=True)  24.4 us
    scatter x1, local copies, waits for them, and re-layouts, on_device(): in_rows = jnp.zeros((total,), jnp.float32).at[row_lists[panel]].set(1.0)  23 us
    all_to_all x3, starting transfers between devices, sent_to_all(): return lax.all_to_all(copies, axis, split_axis=0, concat_axis=0, tiled=True)  15.9 us
    all_to_all x1, starting transfers between devices, on_device(): parts = lax.all_to_all(parts, ROW, split_axis=0, concat_axis=0)  7.87 us
    gather x2, local copies, waits for them, and re-layouts, on_device(): beside = jnp.take(product_cols, row_safe, axis=1).T  5.71 us
  transfers between devices with their start and end apart: 4, of which 4 were waited for; matrix products, arithmetic and copies ran while one was open for 19% of the time, Pallas kernels for 0%

profile of v1, /device:TPU:16, one launch (start us, length us, event | category | flops | bytes accessed | tf_op | source)
XLA Modules:
  0.0 277.5 jit_solution(15970481965888000474)
XLA Ops:
  0.0 0.0 copy-start.4
  0.0 1.8 stack.3
  1.8 7.9 %all-to-all-start = ((f32[16,384,32]{1,2,0:T(8,128)}), f32[16,384,32]{1,2,0:T(8,128)S(1)}, u32[]{:S(2)}, u32[]{:S(2)}) async-start(f32[16,384,32]{1,2,0:T(8,128)} %stack.3), calls=%async_computation | async-start | bytes 1572864 | tf_op jit(solution)/shard_map/all_to_all | solution.py:96
  9.6 0.0 copy-done.4
  9.7 23.0 %scatter_custom_fusion.1 = f32[12288]{0:T(1024)S(1)} fusion(s32[6144]{0:T(1024)S(1)} %bitcast.49, f32[6144]{0:T(1024)S(1)} %broadcast.143, f32[]{:T(128)} %constant.105.clone.1), kind=kCustom, calls=%fused_computation.21 | custom fusion | bytes 49156 | tf_op jit(solution)/shard_map/scatter | solution.py:86
  32.8 2.5 gather_fusion.2
  35.3 0.3 all-to-all-done
  35.6 0.0 copy-start.1
  35.6 0.1 bitcast_multiply_fusion
  35.7 1.2 copy-done.1
  36.9 2.7 negate_bitcast_fusion
  39.6 1.6 copy.27
  41.2 51.8 %all_to_all.45 = f32[32,24,512]{2,1,0:T(8,128)S(1)} all-to-all(f32[32,24,512]{2,1,0:T(8,128)} %bitcast.44), channel_id=1, replica_groups=mesh['row_0'=4,'row_1'=2,'row_2'=2,'col'=32] {'col'}, dimensions={0} | all-to-all | bytes 3145728 | tf_op jit(solution)/shard_map/all_to_all | solution.py:18
  93.0 0.1 reduce_sum.36
  93.1 1.3 broadcast_in_dim.74
  94.4 6.4 %all-to-all-start.2 = ((f32[32,24,512]{2,1,0:T(8,128)}), f32[32,24,512]{2,1,0:T(8,128)S(1)}, u32[]{:S(2)}, u32[]{:S(2)}) async-start(f32[32,24,512]{2,1,0:T(8,128)} %broadcast_in_dim.74), calls=%async_computation.2 | async-start | bytes 3145728 | tf_op jit(solution)/shard_map/all_to_all | solution.py:30
  100.9 39.0 %all-to-all-done.2 = f32[32,24,512]{2,1,0:T(8,128)S(1)} async-done(((f32[32,24,512]{2,1,0:T(8,128)}), f32[32,24,512]{2,1,0:T(8,128)S(1)}, u32[]{:S(2)}, u32[]{:S(2)}) %all-to-all-start.2) | async-done | bytes 1572896 | tf_op jit(solution)/shard_map/all_to_all | solution.py:30
  139.9 0.0 copy-start
  139.9 0.1 dynamic-slice_select_fusion
  140.0 0.1 copy.28
  140.0 1.0 copy-done
  141.1 4.4 %all_to_all.46 = f32[2,8,24,512]{3,2,1,0:T(8,128)S(1)} all-to-all(f32[2,8,24,512]{3,2,1,0:T(8,128)S(1)} %copy.28), channel_id=1, replica_groups=mesh['row_0'=4,'row_1'=2,'row_2'=2,'col'=32] {'row_2'}, dimensions={0} | all-to-all | bytes 1572864 | tf_op jit(solution)/shard_map/all_to_all | solution.py:18
  145.4 0.1 reduce_sum.37
  145.5 24.4 %all_to_all.47 = f32[8,24,512]{2,1,0:T(8,128)S(1)} all-to-all(f32[8,24,512]{2,1,0:T(8,128)S(1)} %reduce_sum.37), channel_id=1, replica_groups=mesh['row_0'=4,'row_1'=2,'row_2'=2,'col'=32] {'row_0','row_1'}, dimensions={0} | all-to-all | bytes 786432 | tf_op jit(solution)/shard_map/all_to_all | solution.py:53
  169.9 0.0 copy-start.3
  169.9 0.8 broadcast_in_dim.76
  170.7 3.5 %all-to-all-start.5 = ((f32[8,24,512]{2,1,0:T(8,128)}), f32[8,24,512]{2,1,0:T(8,128)S(1)}, u32[]{:S(2)}, u32[]{:S(2)}) async-start(f32[8,24,512]{2,1,0:T(8,128)} %broadcast_in_dim.76), calls=%async_computation.5 | async-start | bytes 786432 | tf_op jit(solution)/shard_map/all_to_all | solution.py:30
  174.1 0.1 broadcast_in_dim.71
  174.3 0.0 copy-done.3
  174.3 0.1 bitcast_multiply_fusion.1
  174.4 13.9 %all-to-all-done.5 = f32[8,24,512]{2,1,0:T(8,128)S(1)} async-done(((f32[8,24,512]{2,1,0:T(8,128)}), f32[8,24,512]{2,1,0:T(8,128)S(1)}, u32[]{:S(2)}, u32[]{:S(2)}) %all-to-all-start.5) | async-done | bytes 393248 | tf_op jit(solution)/shard_map/all_to_all | solution.py:30
  188.3 0.1 broadcast_in_dim.77
  188.4 4.4 %all_to_all.48 = f32[2,8,24,512]{3,2,1,0:T(8,128)S(1)} all-to-all(f32[2,8,24,512]{3,2,1,0:T(8,128)S(1)} %broadcast_in_dim.77), channel_id=1, replica_groups=mesh['row_0'=4,'row_1'=2,'row_2'=2,'col'=32] {'row_2'}, dimensions={0} | all-to-all | bytes 1572864 | tf_op jit(solution)/shard_map/all_to_all | solution.py:30
  192.7 0.1 copy.29
  192.8 1.8 convolution_subtract_fusion
  194.6 35.8 %all_to_all.49 = f32[32,16,512]{2,1,0:T(8,128)S(1)} all-to-all(f32[32,16,512]{2,1,0:T(8,128)S(1)} %bitcast.45), channel_id=1, replica_groups=mesh['row_0'=4,'row_1'=2,'row_2'=2,'col'=32] {'col'}, dimensions={0} | all-to-all | bytes 2097152 | tf_op jit(solution)/shard_map/all_to_all | solution.py:18
  230.5 0.1 reduce_sum.39
  230.5 1.1 broadcast_in_dim.78
  231.6 0.0 copy-start.5
  231.6 6.0 %all-to-all-start.8 = ((f32[32,16,512]{2,1,0:T(8,128)}), f32[32,16,512]{2,1,0:T(8,128)S(1)}, u32[]{:S(2)}, u32[]{:S(2)}) async-start(f32[32,16,512]{2,1,0:T(8,128)} %broadcast_in_dim.78), calls=%async_computation.8 | async-start | bytes 2097152 | tf_op jit(solution)/shard_map/all_to_all | solution.py:30
  237.7 0.0 copy-done.5
  237.7 2.6 scatter_custom_fusion
  240.4 2.5 gather_fusion.1
  243.0 4.5 %gather_fusion = s32[768]{0:T(1024)S(1)} fusion(s32[12288]{0:T(1024)S(1)} %scatter_custom_fusion, s32[1024]{0:T(1024)S(1)} %pad_clamp_fusion.3), kind=kCustom, calls=%fused_computation.2 | custom fusion | bytes 9216 | tf_op jit(solution)/shard_map/gather | solution.py:112
  247.4 0.0 copy-start.2
  247.4 4.5 %gather_fusion.5 = f32[768]{0:T(1024)S(1)} fusion(f32[12288]{0:T(1024)S(1)} %scatter_custom_fusion.1, s32[1024]{0:T(1024)S(1)} %pad_clamp_fusion.3), kind=kCustom, calls=%fused_computation.7 | custom fusion | bytes 9216 | tf_op jit(solution)/shard_map/gather | solution.py:116
  251.9 0.0 copy-done.2
  251.9 1.4 copy.34
  253.4 1.9 copy.33
  255.3 2.5 gather_fusion.7
  257.7 0.3 copy.31
  258.0 3.0 %gather_fusion.4 = f32[768,384]{1,0:T(8,128)} fusion(f32[384,512]{0,1:T(8,128)S(1)} %copy.31, s32[1024]{0:T(1024)S(1)} %pad_clamp_fusion.1), kind=kCustom, calls=%fused_computation.6 | custom fusion | bytes 2362368 | tf_op jit(solution)/shard_map/jit(_take)/gather | solution.py:121
  261.0 2.7 copy.32
  263.7 1.6 all-to-all-done.8
  265.3 2.1 gather_fusion.3
  267.5 1.3 broadcast_select_fusion
  268.8 1.9 copy.30
  270.7 2.5 gather_fusion.6
  273.1 3.0 %fusion.1 = f32[768,384]{0,1:T(8,128)S(1)} fusion(f32[768,384]{0,1:T(8,128)} %copy.34, f32[384,768]{1,0:T(8,128)} %gather_fusion.7, f32[384,768]{1,0:T(8,128)} %gather_fusion.6, f32[768,384]{0,1:T(8,128)} %copy.32, pred[384]{0:T(512)(128)(4,1)S(1)} %get-tuple-element.9, pred[768]{0:T(1024)(128)(4,1)S(1)} %get-tuple-element.7, ...), kind=kLoop, calls=%fused_computation.14 | loop fusion | flops 2654208 | bytes 5901696 | tf_op jit(solution)/shard_map/jit(_where)/select_n | solution.py:123
  276.1 1.4 copy.35
  (18 shorter events, 0.2 us)
Async XLA Ops:
  0.0 9.6 %copy-start.4 = (s32[1,6144]{1,0:T(1,128)S(1)}, s32[1,6144]{1,0:T(1,128)}, u32[]{:S(2)}) copy-start(s32[1,6144]{1,0:T(1,128)} %param.11) | copy-start | bytes 73732
  1.8 33.8 %all-to-all-start = ((f32[16,384,32]{1,2,0:T(8,128)}), f32[16,384,32]{1,2,0:T(8,128)S(1)}, u32[]{:S(2)}, u32[]{:S(2)}) async-start(f32[16,384,32]{1,2,0:T(8,128)} %stack.3), calls=%async_computation | async-start | bytes 1572864 | tf_op jit(solution)/shard_map/all_to_all | solution.py:96
  35.6 1.3 copy-start.1
  94.4 45.5 %all-to-all-start.2 = ((f32[32,24,512]{2,1,0:T(8,128)}), f32[32,24,512]{2,1,0:T(8,128)S(1)}, u32[]{:S(2)}, u32[]{:S(2)}) async-start(f32[32,24,512]{2,1,0:T(8,128)} %broadcast_in_dim.74), calls=%async_computation.2 | async-start | bytes 3145728 | tf_op jit(solution)/shard_map/all_to_all | solution.py:30
  139.9 1.2 copy-start
  169.9 4.4 %copy-start.3 = (f32[1,16,512]{2,1,0:T(8,128)S(1)}, f32[1,16,512]{2,1,0:T(8,128)}, u32[]{:S(2)}) copy-start(f32[1,16,512]{2,1,0:T(8,128)} %param.9) | copy-start | bytes 98308
  170.7 17.6 %all-to-all-start.5 = ((f32[8,24,512]{2,1,0:T(8,128)}), f32[8,24,512]{2,1,0:T(8,128)S(1)}, u32[]{:S(2)}, u32[]{:S(2)}) async-start(f32[8,24,512]{2,1,0:T(8,128)} %broadcast_in_dim.76), calls=%async_computation.5 | async-start | bytes 786432 | tf_op jit(solution)/shard_map/all_to_all | solution.py:30
  231.6 6.1 %copy-start.5 = (s32[1,512]{1,0:T(1,128)S(1)}, s32[1,512]{1,0:T(1,128)}, u32[]{:S(2)}) copy-start(s32[1,512]{1,0:T(1,128)} %param.10) | copy-start | bytes 6148
  231.6 33.7 %all-to-all-start.8 = ((f32[32,16,512]{2,1,0:T(8,128)}), f32[32,16,512]{2,1,0:T(8,128)S(1)}, u32[]{:S(2)}, u32[]{:S(2)}) async-start(f32[32,16,512]{2,1,0:T(8,128)} %broadcast_in_dim.78), calls=%async_computation.8 | async-start | bytes 2097152 | tf_op jit(solution)/shard_map/all_to_all | solution.py:30
  247.4 4.5 %copy-start.2 = (f32[768,384]{1,0:T(8,128)S(1)}, f32[768,384]{1,0:T(8,128)}, u32[]{:S(2)}) copy-start(f32[768,384]{1,0:T(8,128)} %param.7) | copy-start | bytes 3538948
